TPU v7x, 32 devices: a whole 2x2x4 slice. The times are simulated.
32 devices in a mesh: dp: 2 (over x), tp: 4 (over z), ep: 4 (over y, core).
Axes of the slice: x: 2, y: 2, z: 4, core: 2. Of those that a mesh axis runs over, the one named last changes fastest.
Arguments:
- tokens: bfloat16 [16384, 1024], P(('dp', 'ep', 'tp')), parts along dimension 0
- expert_ids: int32 [16384, 8], P(('dp', 'ep', 'tp')), parts along dimension 0
- gates: float32 [16384, 8], P(('dp', 'ep', 'tp')), parts along dimension 0
- w_gate: bfloat16 [32, 1024, 512], P('ep', None, 'tp')
- w_up: bfloat16 [32, 1024, 512], P('ep', None, 'tp')
- w_down: bfloat16 [32, 512, 1024], P('ep', 'tp')
Outputs:
- output: bfloat16 [16384, 1024], P(('dp', 'ep', 'tp')), parts along dimension 0
There are 2 independent parts. A program takes and returns all parts, laid end to end along the dimension named above; an argument that names none is the same for every part.
All inputs are finite; a program needn't handle non-finite values.
Results may differ from a plain program's by a relative error of at most 0.001.
Values are sent between devices in bfloat16 or wider.
A program may use at most 1 GiB of HBM per device.

v0:
```python
import jax
import jax.numpy as jnp
from jax import lax
from jax.sharding import PartitionSpec as P


def solution(mesh):
    ep_size = mesh.shape["ep"]
    row_spec = P(("dp", "ep", "tp"), None)

    def local_layer(tokens, expert_ids, gates, w_gate, w_up, w_down):
        top_k = expert_ids.shape[1]
        local_experts = w_gate.shape[0]
        hidden = tokens.shape[1]
        all_tokens = lax.all_gather(tokens, ("ep", "tp"), tiled=True)
        all_ids = lax.all_gather(expert_ids, ("ep", "tp"), tiled=True)
        all_gates = lax.all_gather(gates, ("ep", "tp"), tiled=True)
        group_rows = all_tokens.shape[0]
        load = group_rows * top_k // (local_experts * ep_size)
        local_ids = all_ids.reshape(-1) - lax.axis_index("ep") * local_experts
        is_mine = (local_ids >= 0) & (local_ids < local_experts)
        sort_key = jnp.where(is_mine, local_ids, local_experts)
        order = jnp.argsort(sort_key, stable=True)[: local_experts * load].reshape(local_experts, load)
        row_index = order // top_k
        gate_disp = all_gates.reshape(-1)[order]
        x_disp = all_tokens[row_index]
        hidden_gate = jnp.einsum("ecd,edf->ecf", x_disp, w_gate, preferred_element_type=jnp.float32)
        hidden_up = jnp.einsum("ecd,edf->ecf", x_disp, w_up, preferred_element_type=jnp.float32)
        act_rows = (jax.nn.silu(hidden_gate) * hidden_up).astype(jnp.bfloat16)
        out_rows = jnp.einsum("ecf,efd->ecd", act_rows, w_down, preferred_element_type=jnp.float32)
        weighted = (out_rows * gate_disp[:, :, None]).reshape(-1, hidden)
        partial_sum = jax.ops.segment_sum(weighted, row_index.reshape(-1), num_segments=group_rows)
        own_rows = lax.psum_scatter(partial_sum, ("ep", "tp"), scatter_dimension=0, tiled=True)
        return own_rows.astype(jnp.bfloat16)

    return jax.shard_map(local_layer, mesh=mesh, in_specs=(row_spec, row_spec, row_spec, P("ep", None, "tp"), P("ep", None, "tp"), P("ep", "tp", None)), out_specs=row_spec, check_vma=False)
```

profile of v0, /device:TPU:0, one launch (start us, length us, event | category | flops | bytes accessed | tf_op | source)
XLA Modules:
  0.0 847.5 jit_solution(5461896649249615428)
XLA Ops:
  6.5 0.0 copy-start
  6.5 0.0 copy-start.1
  6.5 0.0 all-gather.2.cloned.1.call-start
  6.5 0.7 all-gather.2.cloned.1.call-update
  7.3 0.0 reduce-scatter.2.cloned.1.call-start
  7.3 39.6 %all_gather.11 = f32[8192,8]{0,1:T(8,128)S(1)} all-gather(f32[512,8]{0,1:T(8,128)} %param.8), channel_id=1, replica_groups=mesh['dp'=2,'tp'=4,'ep'=4] {'ep','tp'}, dimensions={0}, use_global_device_ids=true | all-gather | bytes 278528 | tf_op jit(solution)/shard_map/all_gather | solution.py:17
  46.9 2.6 copy.8
  49.5 3.6 reshape.19
  53.2 0.0 copy-done.1
  53.2 33.6 %all_gather.9 = s32[8192,8]{0,1:T(8,128)S(1)} all-gather(s32[512,8]{0,1:T(8,128)S(1)} %copy-done.1), channel_id=1, replica_groups=mesh['dp'=2,'tp'=4,'ep'=4] {'ep','tp'}, dimensions={0}, use_global_device_ids=true | all-gather | bytes 278528 | tf_op jit(solution)/shard_map/all_gather | solution.py:16
  86.8 2.6 copy.7
  89.4 3.6 sub.17
  93.1 25.4 %sort.17 = (s32[65536]{0:T(1024)}, s32[65536]{0:T(1024)S(1)}) sort(s32[65536]{0:T(1024)S(1)} %and_select_fusion, s32[65536]{0:T(1024)S(1)} %iota.4), dimensions={0}, to_apply=%region_0.1 | sort | flops 1048576 | bytes 1048576 | tf_op jit(solution)/shard_map/jit(argsort)/sort | solution.py:23
  118.6 0.1 fusion.4
  118.7 90.5 %gather_fusion.1 = f32[16384]{0:T(1024)S(1)} fusion(f32[65536]{0:T(1024)S(1)} %reshape.19, s32[16384]{0:T(1024)S(1)} %broadcast_clamp_fusion), kind=kCustom, calls=%fused_computation.1 | custom fusion | bytes 196608 | tf_op jit(solution)/shard_map/gather | solution.py:25
  209.3 0.0 all-gather.2.cloned.1.call-done
  209.3 88.1 %gather_fusion = bf16[16384,1024]{1,0:T(8,128)(2,1)} fusion(bf16[8192,1024]{1,0:T(8,128)(2,1)} %all-gather.2.cloned.1.call-done, s32[16384]{0:T(1024)S(1)} %broadcast_clamp_fusion.1), kind=kCustom, calls=%fused_computation | custom fusion | bytes 67174400 | tf_op jit(solution)/shard_map/gather | solution.py:26
  297.5 17.6 %fusion.8 = f32[8,2048,128]{2,1,0:T(8,128)} fusion(bf16[8,2048,1024]{2,1,0:T(8,128)(2,1)} %bitcast.16, bf16[8,1024,128]{2,1,0:T(8,128)(2,1)} %param.9), kind=kOutput, calls=%fused_computation.24 | convolution fusion | flops 4294967296 | bytes 44040192 | tf_op jit(solution)/shard_map/ecd,edf->ecf/dot_general | solution.py:27
  315.1 0.0 copy-done
  315.1 42.0 %broadcast_multiply_fusion = f32[8,2048,1024]{2,1,0:T(8,128)} fusion(f32[8,2048]{1,0:T(8,128)S(1)} %reshape.30, bf16[8,128,1024]{2,1,0:T(8,128)(2,1)S(1)} %copy-done, f32[8,2048,128]{2,1,0:T(8,128)} %fusion.8, bf16[8,2048,1024]{2,1,0:T(8,128)(2,1)} %bitcast.17, bf16[8,1024,128]{2,1,0:T(8,128)(2,1)} %param.10), kind=kOutput, calls=%fused_computation.3 | convolution fusion | flops 8619294720 | bytes 113311744 | tf_op jit(solution)/shard_map/ecf,efd->ecd/dot_general | solution.py:30
  357.1 153.4 %scatter_custom_fusion = f32[8192,1024]{1,0:T(8,128)} fusion(s32[16384]{0:T(1024)S(1)} %bitcast.20, f32[16384,1024]{1,0:T(8,128)} %bitcast.1, f32[]{:T(128)} %constant.10.clone.1), kind=kCustom, calls=%fused_computation.4 | custom fusion | flops 16777216 | bytes 33554944 | tf_op jit(solution)/shard_map/scatter-add | solution.py:32
  510.5 0.0 reduce-scatter.2.cloned.1.call-update
  510.5 327.4 %reduce-scatter.2.cloned.1.call-done = f32[512,1024]{1,0:T(8,128)} async-done(((f32[8192,1024]{1,0:T(8,128)}), f32[512,1024]{1,0:T(8,128)}) %reduce-scatter.2.cloned.1.call-update) | async-done | bytes 2097168 | tf_op jit(solution)/shard_map/reduce_scatter | solution.py:33
  837.9 2.7 convert_element_type.7
  (11 shorter events, 0.2 us)
Async XLA Ops:
  6.5 308.6 %copy-start = (bf16[8,128,1024]{2,1,0:T(8,128)(2,1)S(1)}, bf16[8,128,1024]{2,1,0:T(8,128)(2,1)}, u32[]{:S(2)}) copy-start(bf16[8,128,1024]{2,1,0:T(8,128)(2,1)} %param.11) | copy-start | bytes 6291460
  6.5 46.6 %copy-start.1 = (s32[512,8]{0,1:T(8,128)S(1)}, s32[512,8]{0,1:T(8,128)}, u32[]{:S(2)}) copy-start(s32[512,8]{0,1:T(8,128)} %param.7) | copy-start | bytes 49156
  6.5 202.8 %all-gather.2.cloned.1.call-start = ((), (), s32[]{:S(2)}) async-start(), calls=%async_computation.1 | async-start | bytes 17825792 | tf_op jit(solution)/shard_map/all_gather | solution.py:15
  7.3 830.7 %reduce-scatter.2.cloned.1.call-start = ((), (), s32[]{:S(2)}) async-start(), calls=%async_computation.2 | async-start | bytes 35651584 | tf_op jit(solution)/shard_map/reduce_scatter | solution.py:33
Sparse Core Ops, SparseCore 0:
  9.5 133.1 all-gather.1
  510.7 327.2 reduce-scatter.1
where the time goes:
time: 848 us; the launch traced here: 847 us
  waiting for transfers between devices  328 us (39%)
  local copies, waits for them, and re-layouts  191 us (23%)
  other arithmetic  182 us (21%)
  blocking collectives  73.3 us (9%)
  matrix products  59.6 us (7%)
  between operations  13.5 us (2%)
    reduce_scatter x1, waiting for transfers between devices, local_layer(): lax.psum_scatter(partial_sum, ('ep', 'tp'), scatter_dimension=0, tiled=True)  327 us
    scatter-add x1, other arithmetic, local_layer(): jax.ops.segment_sum(weighted, row_index.reshape(-1), num_segments=group_r...  153 us
    gather x2, local copies, waits for them, and re-layouts, local_layer(): gate_disp = all_gates.reshape(-1)[order]  90.6 us
    gather x1, local copies, waits for them, and re-layouts, local_layer(): x_disp = all_tokens[row_index]  88.1 us
    dot_general x1, matrix products, local_layer(): jnp.einsum('ecf,efd->ecd', act_rows, w_down, preferred_element_type=jnp.f...  42 us
    all_gather x1, blocking collectives, local_layer(): all_gates = lax.all_gather(gates, ('ep', 'tp'), tiled=True)  39.6 us
    all_gather x1, blocking collectives, local_layer(): all_ids = lax.all_gather(expert_ids, ('ep', 'tp'), tiled=True)  33.6 us
    sort x1, other arithmetic, local_layer(): jnp.argsort(sort_key, stable=True)[:local_experts * load]  25.4 us
  transfers between devices with their start and end apart: 2, of which 1 were waited for; matrix products, arithmetic and copies ran while one was open for 15% of the time, Pallas kernels for 0%

commit v1 on v0

v1 whole, which is shorter than its diff:
```python
import functools

import jax
import jax.numpy as jnp
from jax import lax
from jax.experimental import pallas as pl
from jax.experimental.pallas import tpu as pltpu
from jax.sharding import PartitionSpec as P

MESH = pl.DeviceIdType.MESH
F32 = jnp.float32
BF16 = jnp.bfloat16

Z_STEPS = (15, 16, 16, 17, 20, 24, 28, 32, 36, 40, 44, 48)
X_STEPS = (18, 28, 41, 53)
CHUNKS = 8


def layer_kernel(
    tok_h, gt_h, wg_h, wu_h, wd_h, out_ref,
    tok, gtb, gm, wg, wu, wd, acc, got_a, got_b, got_c,
    loc_sem, tok_ss, tok_rs, own_ss, own_rs, z_ss, q_rs, x_ss, c_ss, c_rs, out_ss, out_rs,
):
    n_own = wg_h.shape[0]
    half = n_own // 2
    rows = tok_h.shape[0]
    hidden = tok_h.shape[1]
    chunk = rows // CHUNKS
    x = lax.axis_index("dp")
    z = lax.axis_index("tp")
    ep = lax.axis_index("ep")
    core = lax.rem(ep, 2)
    to_x = {"dp": 1 - x}
    to_y = {"ep": lax.rem(ep + 2, 4)}
    to_c = {"ep": ep + 1 - 2 * core}
    to_z = {"tp": z + 1 - 2 * lax.rem(z, 2)}
    to_zz = {"tp": lax.rem(z + 2, 4)}

    def rcopy(src, dst, ss, rs, dev):
        return pltpu.make_async_remote_copy(
            src_ref=src, dst_ref=dst, send_sem=ss, recv_sem=rs, device_id=dev, device_id_type=MESH
        )

    bufs = (wg, wu, wd)
    hbm = (wg_h, wu_h, wd_h)

    loc = [
        pltpu.make_async_copy(tok_h, tok.at[0], loc_sem.at[0]),
        pltpu.make_async_copy(gt_h, gtb.at[0], loc_sem.at[1]),
    ] + [pltpu.make_async_copy(hbm[a], bufs[a].at[0, 0], loc_sem.at[2 + a]) for a in range(3)]
    for cp in loc:
        cp.start()

    barrier = pltpu.get_barrier_semaphore()
    for dev in (to_x, to_y, to_c, to_z, to_zz):
        pl.semaphore_signal(barrier, inc=1, device_id=dev, device_id_type=MESH)
    pl.semaphore_wait(barrier, 5)

    tok_y = [rcopy(tok_h, tok.at[1], tok_ss.at[0], tok_rs.at[0], to_y),
             rcopy(gt_h, gtb.at[1], tok_ss.at[1], tok_rs.at[1], to_y)]
    tok_z = [rcopy(tok_h, tok.at[2], tok_ss.at[2], tok_rs.at[2], to_zz),
             rcopy(gt_h, gtb.at[2], tok_ss.at[3], tok_rs.at[3], to_zz)]
    tok_f = [rcopy(tok.at[2], tok.at[3], tok_ss.at[4], tok_rs.at[4], to_y),
             rcopy(gtb.at[2], gtb.at[3], tok_ss.at[5], tok_rs.at[5], to_y)]

    def own_c(i, a):
        return rcopy(hbm[a].at[i], bufs[a].at[0, 1, i], own_ss.at[i, a], own_rs.at[i, a], to_c)

    def over_z(i, a):
        return rcopy(hbm[a].at[x * half + i], bufs[a].at[1, 0, 2 * i], z_ss.at[i, a], q_rs.at[2 * i, a], to_z)

    def over_x(i, a):
        return rcopy(bufs[a].at[1, 0, 2 * i], bufs[a].at[1, 0, 2 * i + 1], x_ss.at[i, a], q_rs.at[2 * i + 1, a], to_x)

    def over_c(q, a):
        return rcopy(bufs[a].at[1, 0, q], bufs[a].at[1, 1, q], c_ss.at[q, a], c_rs.at[q, a], to_c)

    for cp in tok_y + tok_z:
        cp.start()
    for a in range(3):
        own_c(0, a).start()
    for i in range(half):
        for a in range(3):
            over_z(i, a).start()
    for i in range(1, n_own):
        for a in range(3):
            own_c(i, a).start()

    def zero(t, carry):
        acc[pl.ds(t, 1)] = jnp.zeros((1,) + acc.shape[1:], F32)
        return carry

    lax.fori_loop(0, acc.shape[0], zero, 0)

    def gates_of(b):
        part = gtb[b]
        full = jnp.concatenate([part, jnp.zeros((128 - part.shape[0], rows), F32)], axis=0)
        gm[b] = full.T

    for cp in loc:
        cp.wait()
    gates_of(0)

    base = (ep * n_own, (ep + 1 - 2 * core) * n_own)
    lane = lax.broadcasted_iota(jnp.int32, (rows, 128), 1)
    cols = min(256, hidden)

    def step(k, carry):
        s = k // 32
        b = (1 - s) * (k // 8) + s * (3 - k % 4)
        i = (1 - s) * (k % 8) + s * ((k - 32) // 4)
        expert = (1 - s) * i + s * (((x + i) % 2) * half + i // 2)

        @pl.when(k < n_own)
        def _():
            for a in range(3):
                own_c(i, a).wait_recv()

        @pl.when(k == 8)
        def _():
            for cp in tok_y:
                cp.wait_recv()
            gates_of(1)

        for n, at in enumerate(Z_STEPS):
            @pl.when(k == at)
            def _(n=n):
                u, a = n // 3, n % 3
                over_z(u, a).wait_recv()
                over_x(u, a).start()
                over_c(2 * u, a).start()

        @pl.when(k == 16)
        def _():
            for cp in tok_z:
                cp.wait_recv()
            for cp in tok_f:
                cp.start()
            gates_of(2)

        @pl.when(k == 24)
        def _():
            for cp in tok_f:
                cp.wait_recv()
            gates_of(3)

        for u, at in enumerate(X_STEPS):
            @pl.when(k == at)
            def _(u=u):
                for a in range(3):
                    over_x(u, a).wait_recv()
                    over_c(2 * u + 1, a).start()

        @pl.when((k >= 32) & (k % 4 == 0))
        def _():
            for a in range(3):
                over_c((k - 32) // 4, a).wait_recv()

        xb = tok[b]
        gates = gm[b]
        hs, gs = [], []
        for c in range(2):
            w_in = jnp.concatenate([wg[s, c, i], wu[s, c, i]], axis=1)
            both = jnp.dot(xb, w_in, preferred_element_type=F32)
            f = both.shape[1] // 2
            hs.append((jax.nn.silu(both[:, :f]) * both[:, f:]).astype(BF16))
            gs.append(jnp.sum(jnp.where(lane == base[c] + expert, gates, 0.0), axis=1, keepdims=True))
        for t in range(hidden // cols):
            sl = pl.ds(t * cols, cols)
            total = acc[b, :, sl]
            for c in range(2):
                total += gs[c] * jnp.dot(hs[c], wd[s, c, i, :, sl], preferred_element_type=F32)
            acc[b, :, sl] = total

        @pl.when(k == 60)
        def _():
            for j in range(CHUNKS):
                send_a(j).start()

        @pl.when(k == 62)
        def _():
            for j in range(CHUNKS):
                send_c(j).start()

        return carry

    def part(j):
        return pl.ds(j * chunk, chunk)

    def send_a(j):
        return rcopy(acc.at[3, part(j)], got_a.at[part(j)], out_ss.at[0, j], out_rs.at[0, j], to_y)

    def send_b(j):
        return rcopy(acc.at[2, part(j)], got_b.at[part(j)], out_ss.at[1, j], out_rs.at[1, j], to_zz)

    def send_c(j):
        return rcopy(acc.at[1, part(j)], got_c.at[part(j)], out_ss.at[2, j], out_rs.at[2, j], to_y)

    lax.fori_loop(0, 64, step, 0)

    for j in range(CHUNKS):
        send_a(j).wait_recv()
        acc[2, part(j)] = acc[2, part(j)] + got_a[part(j)]
        send_b(j).start()
    for j in range(CHUNKS):
        send_c(j).wait_recv()
        acc[0, part(j)] = acc[0, part(j)] + got_c[part(j)]
    for j in range(CHUNKS):
        send_b(j).wait_recv()
        out_ref[part(j)] = (acc[0, part(j)] + got_b[part(j)]).astype(out_ref.dtype)

    for cp in tok_y + tok_z + tok_f:
        cp.wait_send()
    for a in range(3):
        for i in range(n_own):
            own_c(i, a).wait_send()
            over_c(i, a).wait_send()
        for i in range(half):
            over_z(i, a).wait_send()
            over_x(i, a).wait_send()
    for j in range(CHUNKS):
        send_a(j).wait_send()
        send_b(j).wait_send()
        send_c(j).wait_send()


def solution(mesh):
    row_spec = P(("dp", "ep", "tp"), None)

    def local_layer(tokens, expert_ids, gates, w_gate, w_up, w_down):
        n_own = w_gate.shape[0]
        rows, hidden = tokens.shape
        ff = w_gate.shape[2]
        experts = n_own * mesh.shape["ep"]
        names = lax.broadcasted_iota(jnp.int32, (experts, 1, rows), 0)
        chosen = expert_ids.T[None] == names
        gate_of = jnp.sum(jnp.where(chosen, gates.T[None], 0.0), axis=1)
        any_spec = pl.BlockSpec(memory_space=pl.ANY)
        dma = pltpu.SemaphoreType.DMA
        return pl.pallas_call(
            layer_kernel,
            out_shape=jax.ShapeDtypeStruct((rows, hidden), jnp.bfloat16),
            in_specs=[any_spec] * 5,
            out_specs=pl.BlockSpec(memory_space=pltpu.VMEM),
            scratch_shapes=[
                pltpu.VMEM((4, rows, hidden), BF16),
                pltpu.VMEM((4, experts, rows), F32),
                pltpu.VMEM((4, rows, 128), F32),
                pltpu.VMEM((2, 2, n_own, hidden, ff), BF16),
                pltpu.VMEM((2, 2, n_own, hidden, ff), BF16),
                pltpu.VMEM((2, 2, n_own, ff, hidden), BF16),
                pltpu.VMEM((4, rows, hidden), F32),
                pltpu.VMEM((rows, hidden), F32),
                pltpu.VMEM((rows, hidden), F32),
                pltpu.VMEM((rows, hidden), F32),
                dma((5,)), dma((6,)), dma((6,)),
                dma((n_own, 3)), dma((n_own, 3)),
                dma((n_own // 2, 3)), dma((n_own, 3)), dma((n_own // 2, 3)),
                dma((n_own, 3)), dma((n_own, 3)),
                dma((3, CHUNKS)), dma((3, CHUNKS)),
            ],
            compiler_params=pltpu.CompilerParams(
                collective_id=0, has_side_effects=True, vmem_limit_bytes=66_060_288
            ),
        )(tokens, gate_of, w_gate, w_up, w_down)

    return jax.shard_map(local_layer, mesh=mesh, in_specs=(row_spec, row_spec, row_spec, P("ep", None, "tp"), P("ep", None, "tp"), P("ep", "tp", None)), out_specs=row_spec, check_vma=False)
```

time: 848 us -> 236 us (0.28)
  waiting for transfers between devices: 328 us -> 0 us
  Pallas kernels: 0 us -> 232 us
  local copies, waits for them, and re-layouts: 191 us -> 2.26 us
  other arithmetic: 182 us -> 1.52 us
  blocking collectives: 73.3 us -> 0 us
  matrix products: 59.6 us -> 0 us
  between operations: 13.5 us -> 0.01 us
    reduce_scatter x1 -> x0, waiting for transfers between devices: 327 us -> none  [local_layer(): lax.psum_scatter(partial_sum, ('ep', 'tp'), scatter_dimension=0, tiled=True)]
    pallas_call x0 -> x1, Pallas kernels: none -> 232 us  [local_layer(): pl.pallas_call(layer_kernel, out_shape=jax.ShapeDtypeStruct((rows, hidden...]
    gather x3 -> x0, local copies, waits for them, and re-layouts: 179 us -> none  [the longest x2 90.6 us: local_layer(): gate_disp = all_gates.reshape(-1)[order]]
    scatter-add x1 -> x0, other arithmetic: 153 us -> none  [local_layer(): jax.ops.segment_sum(weighted, row_index.reshape(-1), num_segments=group_r...]
    all_gather x2 -> x0, blocking collectives: 73.3 us -> none  [the longest x1 39.6 us: local_layer(): all_gates = lax.all_gather(gates, ('ep', 'tp'), tiled=True)]
    dot_general x2 -> x0, matrix products: 59.6 us -> none  [the longest x1 42 us: local_layer(): jnp.einsum('ecf,efd->ecd', act_rows, w_down, preferred_element_type=jnp.f...]
    sort x1 -> x0, other arithmetic: 25.4 us -> none  [local_layer(): jnp.argsort(sort_key, stable=True)[:local_experts * load]]
  transfers between devices with their start and end apart: 2 -> 0, of which waited for: 1 -> 0; matrix products, arithmetic and copies ran while one was open for 15% -> 0% of each run, Pallas kernels for 0% -> 0%
where the time goes in v1:
time: 236 us; the launch traced here: 235 us
  Pallas kernels  232 us (98%)
    pallas_call x1, Pallas kernels, local_layer(): pl.pallas_call(layer_kernel, out_shape=jax.ShapeDtypeStruct((rows, hidden...  232 us

profile of v1, /device:TPU:0, one launch (start us, length us, event | category | flops | bytes accessed | tf_op | source)
XLA Modules:
  0.0 235.3 jit_solution(8641929034337262043)
XLA Ops:
  0.0 1.5 select_reduce_fusion.gt_h
  1.5 231.5 %shard_map.64 = bf16[512,1024]{1,0:T(8,128)(2,1)} custom-call(bf16[512,1024]{1,0:T(8,128)(2,1)} %tok_h.1, f32[32,512]{1,0:T(8,128)} %select_reduce_fusion.gt_h, bf16[8,1024,128]{2,1,0:T(8,128)(2,1)} %wg_h.1, bf16[8,1024,128]{2,1,0:T(8,128)(2,1)} %wu_h.1, bf16[8,128,1024]{2,1,0:T(8,128)(2,1)} %wd_h.1), custom_call_target="tpu_custom_call" | custom-call | tf_op jit(solution)/shard_map/pallas_call | solution.py:240
  233.1 2.3 copy.8

commit v2 on v1

v2 whole, which is shorter than its diff:
```python
import functools

import jax
import jax.numpy as jnp
from jax import lax
from jax.experimental import pallas as pl
from jax.experimental.pallas import tpu as pltpu
from jax.sharding import PartitionSpec as P

MESH = pl.DeviceIdType.MESH
F32 = jnp.float32
BF16 = jnp.bfloat16

CHUNKS = 8


def layer_kernel(
    tok_h, gt_h, wg_h, wu_h, wd_h, out_ref,
    tok, gtb, gm, wg, wu, wd, hid, acc, got_a, got_b, got_c,
    loc_sem, tok_ss, tok_rs, own_ss, own_rs, z_ss, q_rs, x_ss, c_ss, c_rs, out_ss, out_rs,
):
    n_own, hidden, ff = wg_h.shape
    half = n_own // 2
    rows = tok_h.shape[0]
    part_rows = rows // 2
    chunks = CHUNKS
    chunk = rows // chunks
    x = lax.axis_index("dp")
    z = lax.axis_index("tp")
    ep = lax.axis_index("ep")
    core = lax.rem(ep, 2)
    to_x = {"dp": 1 - x}
    to_y = {"ep": lax.rem(ep + 2, 4)}
    to_c = {"ep": ep + 1 - 2 * core}
    to_z = {"tp": z + 1 - 2 * lax.rem(z, 2)}
    to_zz = {"tp": lax.rem(z + 2, 4)}
    row_d, row_c, row_b, row_a = 0, rows, 2 * rows, 3 * rows

    def rcopy(src, dst, ss, rs, dev):
        return pltpu.make_async_remote_copy(
            src_ref=src, dst_ref=dst, send_sem=ss, recv_sem=rs, device_id=dev, device_id_type=MESH
        )

    bufs = (wg, wu, wd)
    hbm = (wg_h, wu_h, wd_h)

    loc = [
        pltpu.make_async_copy(tok_h, tok.at[pl.ds(row_d, rows)], loc_sem.at[0]),
        pltpu.make_async_copy(gt_h, gtb.at[0], loc_sem.at[1]),
    ] + [pltpu.make_async_copy(hbm[a], bufs[a].at[0, 0], loc_sem.at[2 + a]) for a in range(3)]
    for cp in loc:
        cp.start()

    barrier = pltpu.get_barrier_semaphore()
    for dev in (to_x, to_y, to_c, to_z, to_zz):
        pl.semaphore_signal(barrier, inc=1, device_id=dev, device_id_type=MESH)
    with jax.named_scope("entry"):
        pl.semaphore_wait(barrier, 5)

    def part(base, p):
        return pl.ds(base + p * part_rows, part_rows)

    tok_y = [rcopy(tok_h, tok.at[pl.ds(row_c, rows)], tok_ss.at[0], tok_rs.at[0], to_y)]
    gat_y = rcopy(gt_h, gtb.at[1], tok_ss.at[1], tok_rs.at[1], to_y)
    gat_z = rcopy(gt_h, gtb.at[2], tok_ss.at[2], tok_rs.at[2], to_zz)
    gat_f = rcopy(gtb.at[2], gtb.at[3], tok_ss.at[3], tok_rs.at[3], to_y)
    tok_z = [rcopy(tok_h.at[part(0, p)], tok.at[part(row_b, p)], tok_ss.at[4 + p], tok_rs.at[4 + p], to_zz)
             for p in range(2)]
    tok_f = [rcopy(tok.at[part(row_b, p)], tok.at[part(row_a, p)], tok_ss.at[6 + p], tok_rs.at[6 + p], to_y)
             for p in range(2)]

    def own_c(i, a):
        return rcopy(hbm[a].at[i], bufs[a].at[0, 1, i], own_ss.at[i, a], own_rs.at[i, a], to_c)

    def over_z(i, a):
        return rcopy(hbm[a].at[x * half + i], bufs[a].at[1, 0, 2 * i], z_ss.at[i, a], q_rs.at[2 * i, a], to_z)

    def over_x(i, a):
        return rcopy(bufs[a].at[1, 0, 2 * i], bufs[a].at[1, 0, 2 * i + 1], x_ss.at[i, a], q_rs.at[2 * i + 1, a], to_x)

    def over_c(q, a):
        return rcopy(bufs[a].at[1, 0, q], bufs[a].at[1, 1, q], c_ss.at[q, a], c_rs.at[q, a], to_c)

    tok_z[0].start()
    gat_z.start()
    tok_y[0].start()
    gat_y.start()
    for a in range(3):
        own_c(0, a).start()
    for i in range(half):
        for a in range(3):
            over_z(i, a).start()
    for i in range(1, n_own):
        for a in range(3):
            own_c(i, a).start()
    tok_z[1].start()

    def zero(t, carry):
        acc[pl.ds(pl.multiple_of(t * rows, rows), rows)] = jnp.zeros((rows, hidden), F32)
        return carry

    lax.fori_loop(0, 4, zero, 0)

    def gates_of(b):
        block = gtb[b]
        full = jnp.concatenate([block, jnp.zeros((128 - block.shape[0], rows), F32)], axis=0)
        gm[pl.ds(b * rows, rows)] = full.T

    with jax.named_scope("loc"):
        for cp in loc:
            cp.wait()
    gates_of(0)

    base = (ep * n_own, (ep + 1 - 2 * core) * n_own)
    cols = min(256, hidden)

    def inner(xb, s, c, i):
        w_in = jnp.concatenate([wg[s, c, i], wu[s, c, i]], axis=1)
        both = jnp.dot(xb, w_in, preferred_element_type=F32)
        return (jax.nn.silu(both[:, :ff]) * both[:, ff:]).astype(BF16)

    def first(r, m, i):
        at = pl.ds(r, m)
        xb = tok[at]
        for c in range(2):
            hid[c, i, at] = inner(xb, 0, c, i)

    def second(r, m, q):
        at = pl.ds(r, m)
        i = ((x + q) % 2) * half + q // 2
        xb = tok[at]
        gates = gm[at]
        lane = lax.broadcasted_iota(jnp.int32, (m, 128), 1)
        hs, gs = [], []
        for c in range(2):
            hs.append(jnp.concatenate([hid[c, i, at], inner(xb, 1, c, q)], axis=1))
            gs.append(jnp.sum(jnp.where(lane == base[c] + i, gates, 0.0), axis=1, keepdims=True))
        for t in range(hidden // cols):
            sl = pl.ds(t * cols, cols)
            total = acc[at, sl]
            for c in range(2):
                w_out = jnp.concatenate([wd[0, c, i, :, sl], wd[1, c, q, :, sl]], axis=0)
                total += gs[c] * jnp.dot(hs[c], w_out, preferred_element_type=F32)
            acc[at, sl] = total

    def first_all(r, m):
        def go(i, carry):
            first(r, m, i)
            return carry

        lax.fori_loop(0, n_own, go, 0)

    def second_all(r, m):
        def go(q, carry):
            second(r, m, q)
            return carry

        lax.fori_loop(0, n_own, go, 0)

    def pass_z(n):
        u, a = n // 3, n % 3
        with jax.named_scope(f"ev_z{n}"):
            over_z(u, a).wait_recv()
        over_x(u, a).start()
        over_c(2 * u, a).start()

    def pass_x(u):
        with jax.named_scope(f"ev_x{u}"):
            for a in range(3):
                over_x(u, a).wait_recv()
                over_c(2 * u + 1, a).start()

    def rows_of(j):
        return pl.ds(j * chunk, chunk)

    def send_a(j):
        return rcopy(acc.at[pl.ds(row_a + j * chunk, chunk)], got_a.at[rows_of(j)], out_ss.at[0, j], out_rs.at[0, j], to_y)

    def send_b(j):
        return rcopy(acc.at[pl.ds(row_b + j * chunk, chunk)], got_b.at[rows_of(j)], out_ss.at[1, j], out_rs.at[1, j], to_zz)

    def send_c(j):
        return rcopy(acc.at[pl.ds(row_c + j * chunk, chunk)], got_c.at[rows_of(j)], out_ss.at[2, j], out_rs.at[2, j], to_y)

    def add_a(j):
        with jax.named_scope(f"late_a{j}"):
            send_a(j).wait_recv()
        at = pl.ds(row_b + j * chunk, chunk)
        acc[at] = acc[at] + got_a[rows_of(j)]
        send_b(j).start()

    def mine(i, carry):
        with jax.named_scope("ev_own"):
            for a in range(3):
                own_c(i, a).wait_recv()
        first(row_d, rows, i)
        return carry

    lax.fori_loop(0, n_own, mine, 0)

    pass_z(0)
    with jax.named_scope("ev_tok_b1"):
        tok_z[0].wait_recv()
        gat_z.wait_recv()
    tok_f[0].start()
    gat_f.start()
    gates_of(2)
    pass_z(1)
    with jax.named_scope("ev_tok_c"):
        tok_y[0].wait_recv()
        gat_y.wait_recv()
    gates_of(1)
    first_all(row_c, rows)
    pass_z(2)
    first_all(row_b, part_rows)
    pass_z(3)
    with jax.named_scope("ev_tok_a1"):
        tok_f[0].wait_recv()
        gat_f.wait_recv()
    gates_of(3)
    first_all(row_a, part_rows)
    pass_x(0)
    pass_z(4)

    def step(q, carry):
        for at, ns, us in ((1, (5,), ()), (2, (6,), ()), (3, (7,), (1,)), (4, (8,), ()), (5, (9,), (2,)),
                           (6, (10, 11), ()), (7, (), (3,))):
            @pl.when(q == at)
            def _(ns=ns, us=us):
                for n in ns:
                    pass_z(n)
                for u in us:
                    pass_x(u)

        with jax.named_scope("ev_q"):
            for a in range(3):
                over_c(q, a).wait_recv()
        second(row_a, part_rows, q)

        @pl.when(q == n_own - 1)
        def _():
            with jax.named_scope("out_a1"):
                for j in range(chunks // 4):
                    send_a(j).start()

        second(row_b, part_rows, q)
        second(row_c, rows, q)
        second(row_d, rows, q)
        return carry

    lax.fori_loop(0, n_own, step, 0)

    with jax.named_scope("ev_tok_b2"):
        tok_z[1].wait_recv()
    tok_f[1].start()
    for j in range(chunks // 4, chunks // 2):
        send_a(j).start()
    first_all(row_b + part_rows, part_rows)
    for j in range(chunks // 4):
        add_a(j)
    second_all(row_b + part_rows, part_rows)
    with jax.named_scope("ev_tok_a2"):
        tok_f[1].wait_recv()
    first_all(row_a + part_rows, part_rows)
    for j in range(chunks // 4, 3 * chunks // 8):
        add_a(j)
    second_all(row_a + part_rows, part_rows)
    with jax.named_scope("out_a2"):
        for j in range(chunks // 2, chunks):
            send_a(j).start()
    for j in range(chunks):
        send_c(j).start()
    for j in range(3 * chunks // 8, chunks):
        add_a(j)
    for j in range(chunks):
        with jax.named_scope(f"late_b{j}"):
            send_b(j).wait_recv()
        with jax.named_scope(f"late_c{j}"):
            send_c(j).wait_recv()
        out_ref[rows_of(j)] = (acc[rows_of(j)] + got_c[rows_of(j)] + got_b[rows_of(j)]).astype(out_ref.dtype)

    for cp in tok_y + tok_z + tok_f + [gat_y, gat_z, gat_f]:
        cp.wait_send()
    for a in range(3):
        for i in range(n_own):
            own_c(i, a).wait_send()
            over_c(i, a).wait_send()
        for i in range(half):
            over_z(i, a).wait_send()
            over_x(i, a).wait_send()
    for j in range(chunks):
        send_a(j).wait_send()
        send_b(j).wait_send()
        send_c(j).wait_send()


def solution(mesh):
    row_spec = P(("dp", "ep", "tp"), None)

    def local_layer(tokens, expert_ids, gates, w_gate, w_up, w_down):
        n_own = w_gate.shape[0]
        rows, hidden = tokens.shape
        ff = w_gate.shape[2]
        experts = n_own * mesh.shape["ep"]
        names = lax.broadcasted_iota(jnp.int32, (experts, 1, rows), 0)
        chosen = expert_ids.T[None] == names
        gate_of = jnp.sum(jnp.where(chosen, gates.T[None], 0.0), axis=1)
        any_spec = pl.BlockSpec(memory_space=pl.ANY)
        dma = pltpu.SemaphoreType.DMA
        return pl.pallas_call(
            layer_kernel,
            out_shape=jax.ShapeDtypeStruct((rows, hidden), jnp.bfloat16),
            in_specs=[any_spec] * 5,
            out_specs=pl.BlockSpec(memory_space=pltpu.VMEM),
            scratch_shapes=[
                pltpu.VMEM((4 * rows, hidden), BF16),
                pltpu.VMEM((4, experts, rows), F32),
                pltpu.VMEM((4 * rows, 128), F32),
                pltpu.VMEM((2, 2, n_own, hidden, ff), BF16),
                pltpu.VMEM((2, 2, n_own, hidden, ff), BF16),
                pltpu.VMEM((2, 2, n_own, ff, hidden), BF16),
                pltpu.VMEM((2, n_own, 4 * rows, ff), BF16),
                pltpu.VMEM((4 * rows, hidden), F32),
                pltpu.VMEM((rows, hidden), F32),
                pltpu.VMEM((rows, hidden), F32),
                pltpu.VMEM((rows, hidden), F32),
                dma((5,)), dma((8,)), dma((8,)),
                dma((n_own, 3)), dma((n_own, 3)),
                dma((n_own // 2, 3)), dma((n_own, 3)), dma((n_own // 2, 3)),
                dma((n_own, 3)), dma((n_own, 3)),
                dma((3, CHUNKS)), dma((3, CHUNKS)),
            ],
            compiler_params=pltpu.CompilerParams(
                collective_id=0, has_side_effects=True, vmem_limit_bytes=66_060_288
            ),
        )(tokens, gate_of, w_gate, w_up, w_down)

    return jax.shard_map(local_layer, mesh=mesh, in_specs=(row_spec, row_spec, row_spec, P("ep", None, "tp"), P("ep", None, "tp"), P("ep", "tp", None)), out_specs=row_spec, check_vma=False)
```

time: 236 us -> 223 us (0.945)
  Pallas kernels: 232 us -> 219 us
    pallas_call x1, Pallas kernels: 232 us -> 219 us  [local_layer(): pl.pallas_call(layer_kernel, out_shape=jax.ShapeDtypeStruct((rows, hidden...]
where the time goes in v2:
time: 223 us
  Pallas kernels  219 us (98%)
  local copies, waits for them, and re-layouts  2.26 us (1%)
    pallas_call x1, Pallas kernels, local_layer(): pl.pallas_call(layer_kernel, out_shape=jax.ShapeDtypeStruct((rows, hidden...  219 us

profile of v2, /device:TPU:0, one launch (start us, length us, event | category | flops | bytes accessed | tf_op | source)
XLA Modules:
  0.0 222.7 jit_solution(7713874043799769177)
XLA Ops:
  0.0 1.5 select_reduce_fusion.gt_h
  1.5 218.9 %shard_map.64 = bf16[512,1024]{1,0:T(8,128)(2,1)} custom-call(bf16[512,1024]{1,0:T(8,128)(2,1)} %tok_h.1, f32[32,512]{1,0:T(8,128)} %select_reduce_fusion.gt_h, bf16[8,1024,128]{2,1,0:T(8,128)(2,1)} %wg_h.1, bf16[8,1024,128]{2,1,0:T(8,128)(2,1)} %wu_h.1, bf16[8,128,1024]{2,1,0:T(8,128)(2,1)} %wd_h.1), custom_call_target="tpu_custom_call" | custom-call | tf_op jit(solution)/shard_map/pallas_call | solution.py:310
  220.4 2.3 %copy.8 = bf16[512,1024]{1,0:T(8,128)(2,1)} copy(bf16[512,1024]{1,0:T(8,128)(2,1)} %shard_map.64) | data formatting | bytes 2097152
